TPU v7x, 256 devices: a whole 4x4x8 slice. The times are simulated.
256 devices in a mesh: ta: 4 (over x), ha: 8 (over z_hi, core), wa: 8 (over z_lo, y).
Axes of the slice: x: 4, y: 4, z: 8 (z_hi: 4, z_lo: 2; z = z_hi * 2 + z_lo), core: 2. Of those that a mesh axis runs over, the one named last changes fastest.
Arguments:
- tokens: bfloat16 [1, 16, 64, 64, 1024], P(None, 'ta', 'ha', 'wa'), may hold values from -40 to 40
- norm_gain: float32 [4, 1024], replicated, may hold values from 0.25 to 1.75
- qkv_weight: bfloat16 [3, 1024, 3, 1024], P(None, None, None, 'ta'), may hold values from -0.1875 to 0.1875
- qk_gain: float32 [3, 2, 64], replicated, may hold values from 0.25 to 1.75
- out_weight: bfloat16 [3, 1024, 1024], P(None, 'ta'), may hold values from -0.1875 to 0.1875
- ffn_in: bfloat16 [1024, 2, 2048], P(None, None, 'ta'), may hold values from -0.1875 to 0.1875
- ffn_out: bfloat16 [2048, 1024], P('ta'), may hold values from -0.125 to 0.125
Outputs:
- layer_out: bfloat16 [1, 16, 64, 64, 1024], P(None, 'ta', 'ha', 'wa')
All inputs are finite; a program needn't handle non-finite values.
Results may differ from a plain program's by a relative error of at most 0.015.
Values may be sent and summed in bfloat16 or wider, within the bound.
A program may use at most 192 MiB of HBM per device.

v0:
```python
import functools

import jax
import jax.numpy as jnp
from jax import lax
from jax.experimental import pallas as pl
from jax.experimental.pallas import tpu as pltpu
from jax.sharding import PartitionSpec as P

MESH = pl.DeviceIdType.MESH
BF16, F32 = jnp.bfloat16, jnp.float32
ROWS = 256
UNIT = 128
D = 1024


def place(x, y, z, k):
    return {"ta": x, "ha": (z // 2) * 2 + k, "wa": (z % 2) * 4 + y}


def rows(start, size):
    return pl.ds(pl.multiple_of(start, size), size)


def dot_t(a, b):
    return lax.dot_general(a, b, (((1,), (1,)), ((), ())), preferred_element_type=F32)


def dot(a, b):
    return jnp.dot(a, b, preferred_element_type=F32)


def rms(stream, gain_row):
    return stream * lax.rsqrt(jnp.mean(stream * stream, axis=-1, keepdims=True) + 1e-6) * gain_row


def iotas(shape):
    return lax.broadcasted_iota(jnp.int32, shape, 0), lax.broadcasted_iota(jnp.int32, shape, 1)


def one_hot(source_of):
    out, into = iotas((ROWS, ROWS))
    return jnp.where(source_of(out) == into, 1.0, 0.0).astype(BF16)


def kernel(
    tok,
    attn_src,
    mlp_src,
    norm_gain,
    qk_gain,
    out_ref,
    w_attn,
    w_mlp,
    arrived,
    leaving,
    stream,
    normed,
    partial,
    partial_in,
    qkv,
    heads,
    mask,
    w_send,
    w_recv,
    own_sem,
    t_send,
    t_recv,
    p_send,
    p_recv,
):
    x = lax.axis_index("ta")
    h = lax.axis_index("ha")
    w = lax.axis_index("wa")
    z_hi, k, z_lo, y = h // 2, h % 2, w // 4, w % 4
    z = z_hi * 2 + z_lo
    par = z_lo
    partner = place(x, y, z, 1 - k)

    def w_ref(p, q, start, size):
        if p < 3:
            return w_attn.at[p, :, rows(start, UNIT) if size == UNIT else pl.ds(start, size), rows(q * 128, 128)]
        return w_mlp.at[:, rows(start, UNIT) if size == UNIT else pl.ds(start, size), rows(q * 256, 256)]

    def src_ref(p, start, size):
        return attn_src.at[p, :, pl.ds(start, size), :] if p < 3 else mlp_src.at[:, pl.ds(start, size), :]

    def w_copy(p, d, kind, src, dst, device, send_index):
        return pltpu.make_async_remote_copy(
            src_ref=src,
            dst_ref=dst,
            send_sem=w_send.at[p, send_index],
            recv_sem=w_recv.at[p, d, kind],
            device_id=device,
            device_id_type=MESH,
        )

    def unit_start(kind_start):
        return pl.multiple_of(kind_start, UNIT)

    gamma = pl.multiple_of(512 + par * 256, 256)
    other = pl.multiple_of(512 + (1 - par) * 256, 256)

    def x_copies(p):
        out = []
        for e in (1, 3, 2):
            peer = place((x + e) % 4, y, z, k)
            for kind, start, size in ((0, unit_start(y * UNIT), UNIT), (1, gamma, 256)):
                out.append(
                    w_copy(p, 4 - e, kind, src_ref(p, start, size), w_ref(p, x, start, size), peer, (e - 1) * 2 + kind)
                )
        return out

    def y_copies(p, d):
        q = (x + d) % 4
        block = w_ref(p, q, unit_start(y * UNIT), UNIT)
        return [
            w_copy(p, d, 1 + (4 - e), block, block, place(x, (y + e) % 4, z, k), 6 + (d - 1) * 5 + e - 1)
            for e in (1, 3, 2)
        ]

    def z_copies(p, d):
        q = (x + d) % 4
        first = w_ref(p, q, unit_start(gamma), UNIT)
        second = w_ref(p, q, unit_start(gamma + UNIT), UNIT)
        up, down = place(x, y, (z + 1) % 8, k), place(x, y, (z + 7) % 8, k)
        return [
            w_copy(p, d, 5, first, first, up, 6 + (d - 1) * 5 + 3),
            w_copy(p, d, 6, second, second, down, 6 + (d - 1) * 5 + 4),
        ]

    def w_wait(p, d, kind, start, size):
        block = w_ref(p, (x + d) % 4, start, size)
        w_copy(p, d, kind, block, block, partner, 0).wait_recv()

    def own_copy(p):
        dst = w_attn.at[p, :, :, rows(x * 128, 128)] if p < 3 else w_mlp.at[:, :, rows(x * 256, 256)]
        return pltpu.make_async_copy(attn_src.at[p] if p < 3 else mlp_src, dst, own_sem.at[p])

    def forward(p):
        for d in (1, 3, 2):
            w_wait(p, d, 0, unit_start(y * UNIT), UNIT)
            for copy in y_copies(p, d):
                copy.start()
            w_wait(p, d, 1, gamma, 256)
            for copy in z_copies(p, d):
                copy.start()

    def weights_in(p):
        own_copy(p).wait()
        for d in (1, 3, 2):
            for slot in (1, 2, 3):
                w_wait(p, d, 1 + slot, unit_start(((y + slot) % 4) * UNIT), UNIT)
            w_wait(p, d, 5, unit_start(other), UNIT)
            w_wait(p, d, 6, unit_start(other + UNIT), UNIT)

    def t_copy(stage, index, src, dst, device):
        return pltpu.make_async_remote_copy(
            src_ref=src,
            dst_ref=dst,
            send_sem=t_send.at[stage, index],
            recv_sem=t_recv.at[stage, index],
            device_id=device,
            device_id_type=MESH,
        )

    def copies0():
        out = []
        for d in range(1, 8):
            to = (w + d) % 8
            start = (to % 4) * 64 + (to // 4) * 32
            out.append(
                t_copy(0, d, tok.at[rows(start, 32), :], arrived.at[0, rows(w * 32, 32), :], {"ta": x, "ha": h, "wa": to})
            )
        return out

    def waits0():
        for d in range(1, 8):
            block = arrived.at[0, rows(((w + 8 - d) % 8) * 32, 32), :]
            t_copy(0, d, block, block, partner).wait_recv()

    own_rows = pltpu.make_async_copy(
        tok.at[rows(y * 64 + z_lo * 32, 32), :], arrived.at[0, rows(w * 32, 32), :], own_sem.at[4]
    )

    j = z * 2 + k
    group = z_hi * 4 + k * 2 + z_lo

    def copies1():
        out = []
        for d in range(1, 16):
            to = (j + d) % 16
            to_z, to_k = to // 2, to % 2
            block = (to_z % 2) * 8 + (to_z // 2) * 2 + to_k
            out.append(
                t_copy(
                    1, d, leaving.at[0, rows(block * 16, 16), :], arrived.at[1, rows(group * 16, 16), :], place(x, y, to_z, to_k)
                )
            )
        return out

    def waits1():
        for d in range(1, 16):
            at = (j + 16 - d) % 16
            at_z, at_k = at // 2, at % 2
            slot = (at_z // 2) * 4 + at_k * 2 + at_z % 2
            block = arrived.at[1, rows(slot * 16, 16), :]
            t_copy(1, d, block, block, partner).wait_recv()

    f = x * 4 + y

    def copies2():
        out = []
        for d in range(1, 16):
            to = (f + d) % 16
            to_x, to_y = to // 4, to % 4
            block = to_y * 4 + to_x
            out.append(
                t_copy(2, d, leaving.at[1, rows(block * 16, 16), :], arrived.at[2, rows(f * 16, 16), :], place(to_x, to_y, z, k))
            )
        return out

    def waits2():
        for d in range(1, 16):
            block = arrived.at[2, rows(((f + 16 - d) % 16) * 16, 16), :]
            t_copy(2, d, block, block, partner).wait_recv()

    slot3 = (x % 2) * 8 + z_hi * 2 + k
    at_home = jnp.logical_and(z_hi == y, k == x // 2)

    def copies3():
        out = []
        for dx in range(4):
            for dy in range(4):
                to_x, to_y = (x + dx) % 4, (y + dy) % 4
                copy = pltpu.make_async_remote_copy(
                    src_ref=leaving.at[2, rows((to_x * 4 + to_y) * 16, 16), :],
                    dst_ref=arrived.at[3, rows(slot3 * 16, 16), :],
                    send_sem=t_send.at[3, dx * 4 + dy],
                    recv_sem=t_recv.at[3, slot3],
                    device_id=place(to_x, to_y, y * 2 + z_lo, x // 2),
                    device_id_type=MESH,
                )
                out.append((dx == 0 and dy == 0, copy))
        return out

    def waits3():
        for slot in range(16):

            @pl.when(jnp.logical_not(jnp.logical_and(at_home, slot3 == slot)))
            def _():
                block = arrived.at[3, slot * 16 : slot * 16 + 16, :]
                t_copy(3, slot, block, block, partner).wait_recv()

    def pair_copy(p, index, src, dst):
        return pltpu.make_async_remote_copy(
            src_ref=src,
            dst_ref=dst,
            send_sem=p_send.at[p, index],
            recv_sem=p_recv.at[p, index],
            device_id=partner,
            device_id_type=MESH,
        )

    def share_copy(p):
        return pair_copy(p, 0, normed.at[p, 0], normed.at[p, 1])

    def return_copy(p):
        return pair_copy(p, 1, partial.at[p], partial_in.at[p])

    lane = lax.broadcasted_iota(jnp.int32, (1, 128), 1)
    left = lane < 64

    def head_sums():
        a, b = iotas((256, 256))
        return jnp.where(a // 64 == b // 64, 1.0 / 64.0, 0.0).astype(BF16)

    def project(p, s):
        tokens = normed[p, s]
        for t in range(3):
            for half in range(2):
                cols = slice(half * 256, half * 256 + 256)
                value = dot(tokens, w_attn[p, t, :, cols])
                if t < 2:
                    mean = dot((value * value).astype(BF16), head_sums())
                    value = value * lax.rsqrt(mean + 1e-6) * qk_gain[p, t : t + 1, :]
                qkv[s, t, :, cols] = value.astype(BF16)

    def attend(p, s):
        def pair(i, carry):
            cols = rows(i * 128, 128)
            queries, key_rows = qkv[s, 0, :, cols], qkv[s, 1, :, cols]
            values = jnp.concatenate([qkv[s, 2, :, cols], jnp.ones((ROWS, 128), BF16)], axis=1)
            results = []
            for side in range(2):
                mine = jnp.where(left if side == 0 else jnp.logical_not(left), queries, jnp.zeros_like(queries))
                weights = jnp.exp(dot_t(mine, key_rows)).astype(BF16) * mask[...]
                summed = dot(weights, values)
                results.append(summed[:, :128] / summed[:, 128:])
            heads[s, :, cols] = jnp.where(left, results[0], results[1]).astype(BF16)
            return carry

        lax.fori_loop(0, 4, pair, 0)
        return dot_t(heads[s], w_attn[p, 3])

    def attention(p):
        share_copy(p).start()
        weights_in(p)
        project(p, 0)
        share_copy(p).wait_recv()
        project(p, 1)
        partial[p] = attend(p, 1).astype(BF16)
        return_copy(p).start()
        stream[...] = stream[...] + attend(p, 0)
        return_copy(p).wait_recv()
        stream[...] = stream[...] + partial_in[p].astype(F32)

    def mlp(s):
        tokens = normed[3, s]
        for part in range(4):
            cols = slice(part * 256, part * 256 + 256)
            gate = dot(tokens, w_mlp[0, :, cols])
            up = dot(tokens, w_mlp[1, :, cols])
            qkv[part // 2, part % 2, :, 0:256] = (gate / (1.0 + jnp.exp(-gate)) * up).astype(BF16)
        hidden = jnp.concatenate([qkv[part // 2, part % 2, :, 0:256] for part in range(4)], axis=1)
        return dot_t(hidden, w_mlp[2])

    for copy in copies0():
        copy.start()
    own_rows.start()
    for copy in x_copies(0):
        copy.start()
    for p in range(4):
        own_copy(p).start()
    for copy in x_copies(1):
        copy.start()

    a, b = iotas((ROWS, ROWS))
    mask[...] = jnp.where((a // 8) % 4 == (b // 8) % 4, 1.0, 0.0).astype(BF16)
    own_rows.wait()
    waits0()
    stream[...] = arrived[0].astype(F32)
    normed[0, 0] = rms(stream[...], norm_gain[0:1, :]).astype(BF16)
    forward(0)
    for copy in x_copies(2):
        copy.start()
    attention(0)

    order = one_hot(lambda o: ((o // 128) * 4 + o % 4) * 32 + ((o // 4) % 4) * 8 + (o // 16) % 8)
    leaving[0] = dot(order, stream[...].astype(BF16)).astype(BF16)
    for copy in copies1():
        copy.start()
    own_block = z_lo * 8 + z_hi * 2 + k
    arrived[1, rows(group * 16, 16), :] = leaving[0, rows(own_block * 16, 16), :]
    a, b = iotas((ROWS, ROWS))
    mask[...] = jnp.where(a % 4 == b % 4, 1.0, 0.0).astype(BF16)
    forward(1)
    for copy in x_copies(3):
        copy.start()
    waits1()
    stream[...] = arrived[1].astype(F32)
    normed[1, 0] = rms(stream[...], norm_gain[1:2, :]).astype(BF16)
    attention(1)

    leaving[1] = stream[...].astype(BF16)
    for copy in copies2():
        copy.start()
    arrived[2, rows(f * 16, 16), :] = leaving[1, rows((y * 4 + x) * 16, 16), :]
    a, b = iotas((ROWS, ROWS))
    mask[...] = jnp.where(jnp.logical_and(a % 16 == b % 16, b // 16 <= a // 16), 1.0, 0.0).astype(BF16)
    forward(2)
    waits2()
    stream[...] = arrived[2].astype(F32)
    normed[2, 0] = rms(stream[...], norm_gain[2:3, :]).astype(BF16)
    forward(3)
    attention(2)

    normed[3, 0] = rms(stream[...], norm_gain[3:4, :]).astype(BF16)
    share_copy(3).start()
    weights_in(3)
    share_copy(3).wait_recv()
    partial[3] = mlp(1).astype(BF16)
    return_copy(3).start()
    stream[...] = stream[...] + mlp(0)
    return_copy(3).wait_recv()
    stream[...] = stream[...] + partial_in[3].astype(F32)

    order = one_hot(lambda o: ((o // 64) * 4 + (o // 4) % 4) * 16 + (o % 4) * 4 + (o // 16) % 4)
    leaving[2] = dot(order, stream[...].astype(BF16)).astype(BF16)
    for maybe_self, copy in copies3():
        if maybe_self:

            @pl.when(jnp.logical_not(at_home))
            def _():
                copy.start()

            @pl.when(at_home)
            def _():
                arrived[3, rows(slot3 * 16, 16), :] = leaving[2, rows(f * 16, 16), :]

        else:
            copy.start()
    waits3()
    order = one_hot(lambda o: (((o // 32) % 2) * 8 + o % 8) * 16 + (o // 64) * 4 + (o // 8) % 4)
    out_ref[...] = dot(order, arrived[3]).astype(BF16)

    for copy in copies0() + copies1() + copies2():
        copy.wait_send()
    for maybe_self, copy in copies3():
        if maybe_self:

            @pl.when(jnp.logical_not(at_home))
            def _():
                copy.wait_send()

        else:
            copy.wait_send()
    for p in range(4):
        for copy in x_copies(p):
            copy.wait_send()
        for d in (1, 3, 2):
            for copy in y_copies(p, d) + z_copies(p, d):
                copy.wait_send()
        share_copy(p).wait_send()
        return_copy(p).wait_send()


def local(tokens, norm_gain, qkv_weight, qk_gain, out_weight, ffn_in, ffn_out):
    k = lax.axis_index("ha") % 2
    qkv_half = lax.dynamic_slice_in_dim(qkv_weight, k * 128, 128, 3).transpose(0, 2, 1, 3)
    out_half = lax.dynamic_slice_in_dim(out_weight, k * 128, 128, 1).transpose(0, 2, 1)
    attn_src = jnp.concatenate([qkv_half, out_half[:, None]], axis=1)
    in_half = lax.dynamic_slice_in_dim(ffn_in, k * 256, 256, 2).transpose(1, 0, 2)
    down_half = lax.dynamic_slice_in_dim(ffn_out, k * 256, 256, 0).T
    mlp_src = jnp.concatenate([in_half, down_half[None]], axis=0)
    gains = jnp.tile(qk_gain * jnp.array([0.125, 1.0], F32)[None, :, None], (1, 1, 4))
    vmem, hbm = pl.BlockSpec(memory_space=pltpu.VMEM), pl.BlockSpec(memory_space=pl.ANY)
    result = pl.pallas_call(
        kernel,
        out_shape=jax.ShapeDtypeStruct((ROWS, D), BF16),
        in_specs=[hbm, hbm, hbm, vmem, vmem],
        out_specs=vmem,
        scratch_shapes=[
            pltpu.VMEM((3, 4, D, 512), BF16),
            pltpu.VMEM((3, D, D), BF16),
            pltpu.VMEM((4, ROWS, D), BF16),
            pltpu.VMEM((3, ROWS, D), BF16),
            pltpu.VMEM((ROWS, D), F32),
            pltpu.VMEM((4, 2, ROWS, D), BF16),
            pltpu.VMEM((4, ROWS, D), BF16),
            pltpu.VMEM((4, ROWS, D), BF16),
            pltpu.VMEM((2, 3, ROWS, 512), BF16),
            pltpu.VMEM((2, ROWS, 512), BF16),
            pltpu.VMEM((ROWS, ROWS), BF16),
            pltpu.SemaphoreType.DMA((4, 21)),
            pltpu.SemaphoreType.DMA((4, 4, 7)),
            pltpu.SemaphoreType.DMA((5,)),
            pltpu.SemaphoreType.DMA((4, 16)),
            pltpu.SemaphoreType.DMA((4, 16)),
            pltpu.SemaphoreType.DMA((4, 2)),
            pltpu.SemaphoreType.DMA((4, 2)),
        ],
        compiler_params=pltpu.CompilerParams(has_side_effects=True, vmem_limit_bytes=60 * 2**20),
    )(tokens.reshape(ROWS, D), attn_src, mlp_src, norm_gain, gains)
    return result.reshape(tokens.shape)


def solution(mesh):
    return jax.shard_map(
        local,
        mesh=mesh,
        in_specs=(
            P(None, "ta", "ha", "wa", None),
            P(),
            P(None, None, None, "ta"),
            P(),
            P(None, "ta", None),
            P(None, None, "ta"),
            P("ta", None),
        ),
        out_specs=P(None, "ta", "ha", "wa", None),
        check_vma=False,
    )
```

profile of v0, /device:TPU:6, one launch (start us, length us, event | category | flops | bytes accessed | tf_op | source)
XLA Modules:
  0.0 197.2 jit_solution(5424508312119670703)
XLA Ops:
  0.0 0.0 copy-start
  0.0 0.0 copy-start.1
  0.0 3.4 %dynamic-slice_bitcast_fusion = bf16[3,3,1024,128]{3,2,1,0:T(8,128)(2,1)} fusion(bf16[3,1024,3,256]{3,1,2,0:T(8,128)(2,1)} %param.10, s32[]{:T(128)S(6)} %select_n.16), kind=kLoop, calls=%fused_computation.1 | loop fusion | bytes 4718596 | tf_op jit(solution)/shard_map/transpose | solution.py:430
  3.4 0.0 copy-done.1
  3.4 0.9 constant_dynamic-slice_fusion.2
  4.4 1.5 copy.12
  5.9 3.6 %pad_maximum_fusion.attn_src = bf16[3,4,1024,128]{3,2,1,0:T(8,128)(2,1)} fusion(bf16[3,1,1024,128]{3,2,1,0:T(8,128)(2,1)S(1)} %bitcast.14, bf16[3,3,1024,128]{3,2,1,0:T(8,128)(2,1)} %dynamic-slice_bitcast_fusion), kind=kLoop, calls=%fused_computation | loop fusion | flops 1572864 | bytes 6291456 | tf_op jit(solution)/shard_map/concatenate | solution.py:432
  9.5 0.0 copy-done
  9.5 0.7 constant_dynamic-slice_fusion.1
  10.2 0.1 copy.16
  10.3 1.9 constant_dynamic-slice_fusion
  12.2 0.0 copy-start.2
  12.2 0.0 copy-start.3
  12.2 2.1 %copy.14 = bf16[256,1024]{0,1:T(8,128)(2,1)} copy(bf16[256,1024]{1,0:T(8,128)(2,1)} %constant_dynamic-slice_fusion) | data formatting | bytes 1048576
  14.3 2.3 %pad_maximum_fusion.1.mlp_src = bf16[3,1024,256]{2,1,0:T(8,128)(2,1)} fusion(bf16[1,1024,256]{2,1,0:T(8,128)(2,1)} %bitcast.16, bf16[2,1024,256]{2,1,0:T(8,128)(2,1)S(1)} %bitcast.13), kind=kLoop, calls=%fused_computation.2 | loop fusion | flops 786432 | bytes 3145728 | tf_op jit(solution)/shard_map/concatenate | solution.py:435
  16.6 0.0 copy-done.2
  16.6 0.0 copy-done.3
  16.6 0.1 broadcast_multiply_fusion
  16.7 0.7 tile.10.qk_gain
  17.4 177.9 %shard_map.82 = bf16[256,1024]{1,0:T(8,128)(2,1)} custom-call(bf16[256,1024]{1,0:T(8,128)(2,1)} %bitcast.17, bf16[3,4,1024,128]{3,2,1,0:T(8,128)(2,1)} %pad_maximum_fusion.attn_src, bf16[3,1024,256]{2,1,0:T(8,128)(2,1)} %pad_maximum_fusion.1.mlp_src, f32[4,1024]{1,0:T(4,128)} %norm_gain.1, f32[3,2,256]{2,1,0:T(2,128)} %tile.10.qk_gain), custom_call_target="tpu_custom_call" | custom-call | tf_op jit(solution)/shard_map/pallas_call | solution.py:438
  195.3 1.9 copy.18
  (1 shorter events, 0.0 us)
Async XLA Ops:
  0.0 9.5 %copy-start = (bf16[1024,2,512]{2,1,0:T(2,128)(2,1)S(1)}, bf16[1024,2,512]{2,1,0:T(2,128)(2,1)}, u32[]{:S(2)}) copy-start(bf16[1024,2,512]{2,1,0:T(2,128)(2,1)} %param.13) | copy-start | bytes 6291460
  0.0 3.4 %copy-start.1 = (bf16[3,256,1024]{2,1,0:T(8,128)(2,1)S(1)}, bf16[3,256,1024]{2,1,0:T(8,128)(2,1)}, u32[]{:S(2)}) copy-start(bf16[3,256,1024]{2,1,0:T(8,128)(2,1)} %param.12) | copy-start | bytes 4718596
  12.2 4.4 %copy-start.2 = (f32[3,2,64]{2,1,0:T(2,128)S(1)}, f32[3,2,64]{2,1,0:T(2,128)}, u32[]{:S(2)}) copy-start(f32[3,2,64]{2,1,0:T(2,128)} %param.11) | copy-start | bytes 4612
  12.2 4.4 %copy-start.3 = (f32[2]{0:T(128)S(1)}, f32[2]{0:T(128)}, u32[]{:S(2)}) copy-start(f32[2]{0:T(128)} %constant.27.clone) | copy-start | bytes 28
where the time goes:
time: 200 us; the launch traced here: 197 us
  Pallas kernels  178 us (89%)
  local copies, waits for them, and re-layouts  13.3 us (7%)
  other arithmetic  5.99 us (3%)
    pallas_call x1, Pallas kernels, local(): pl.pallas_call(kernel, out_shape=jax.ShapeDtypeStruct((ROWS, D), BF16), i...  178 us
    unnamed x12, local copies, waits for them, and re-layouts  5.62 us

commit v1 on v0

v1 whole, which is shorter than its diff:
```python
import functools

import jax
import jax.numpy as jnp
from jax import lax
from jax.experimental import pallas as pl
from jax.experimental.pallas import tpu as pltpu
from jax.sharding import PartitionSpec as P

MESH = pl.DeviceIdType.MESH
BF16, F32 = jnp.bfloat16, jnp.float32
ROWS = 256
UNIT = 128
D = 1024


def place(x, y, z, k):
    return {"ta": x, "ha": (z // 2) * 2 + k, "wa": (z % 2) * 4 + y}


def rows(start, size):
    return pl.ds(pl.multiple_of(start, size), size)


def dot_t(a, b):
    return lax.dot_general(a, b, (((1,), (1,)), ((), ())), preferred_element_type=F32)


def dot(a, b):
    return jnp.dot(a, b, preferred_element_type=F32)


def rms(stream, gain_row):
    return stream * lax.rsqrt(jnp.mean(stream * stream, axis=-1, keepdims=True) + 1e-6) * gain_row


def iotas(shape):
    return lax.broadcasted_iota(jnp.int32, shape, 0), lax.broadcasted_iota(jnp.int32, shape, 1)


def one_hot(source_of):
    out, into = iotas((ROWS, ROWS))
    return jnp.where(source_of(out) == into, 1.0, 0.0).astype(BF16)


def kernel(
    tok,
    qkv_src,
    out_src,
    in_src,
    down_src,
    norm_gain,
    qk_gain,
    out_ref,
    w_attn,
    w_out,
    w_in,
    w_down,
    arrived,
    leaving,
    stream,
    normed,
    partial,
    partial_in,
    qkv,
    heads,
    hidden,
    mask,
    w_send,
    w_recv,
    own_sem,
    t_send,
    t_recv,
    p_send,
    p_recv,
    hello,
):
    x = lax.axis_index("ta")
    h = lax.axis_index("ha")
    w = lax.axis_index("wa")
    z_hi, k, z_lo, y = h // 2, h % 2, w // 4, w % 4
    z = z_hi * 2 + z_lo
    phase = z_hi + 2 * z_lo + k
    partner = place(x, y, z, 1 - k)

    def both(p, d, start, size):
        if p < 3:
            return w_attn.at[p, d, :, pl.ds(start, size), :], w_out.at[p, d * 128 : d * 128 + 128, pl.ds(start, size)]
        return w_in.at[d, :, pl.ds(start, size), :], w_down.at[d * 256 : d * 256 + 256, pl.ds(start, size)]

    def both_src(p, start, size):
        if p < 3:
            return (
                qkv_src.at[p, :, pl.ds(start, size), rows(k * 128, 128)],
                out_src.at[p, rows(k * 128, 128), pl.ds(start, size)],
            )
        return (
            in_src.at[:, pl.ds(start, size), rows(k * 256, 256)],
            down_src.at[rows(k * 256, 256), pl.ds(start, size)],
        )

    def w_copies(p, d, kind, src, dst, device):
        return [
            pltpu.make_async_remote_copy(
                src_ref=a,
                dst_ref=b,
                send_sem=w_send.at[p],
                recv_sem=w_recv.at[p, d, kind],
                device_id=device,
                device_id_type=MESH,
            )
            for a, b in zip(src, dst)
        ]

    def w_total(p, d, kind, units):
        block = w_down.at[0 : (64 if p < 3 else 96) * units, :]
        return w_copies(p, d, kind, [block], [block], partner)[0]

    def w_wait(p, d, kind, units):
        w_total(p, d, kind, units).wait_recv()

    def unit(start):
        return pl.multiple_of(start, UNIT)

    gamma = pl.multiple_of(512 + z_lo * 256, 256)

    def x_send(p, kind, steps=(1, 3, 2)):
        for e in steps:
            peer = place((x + e) % 4, y, z, k)
            start, size = ((unit(y * UNIT), UNIT), (gamma, 256))[kind]
            for copy in w_copies(p, 4 - e, kind, both_src(p, start, size), both(p, 4 - e, start, size), peer):
                copy.start()

    def forward_y(p, *quarters):
        for d in quarters:
            w_wait(p, d, 0, 1)
            block = both(p, d, unit(y * UNIT), UNIT)
            for e in (1, 3, 2):
                for copy in w_copies(p, d, 2, block, block, place(x, (y + e) % 4, z, k)):
                    copy.start()

    def forward_z(p, *quarters):
        for d in quarters:
            w_wait(p, d, 1, 2)
            for side, step in ((0, 1), (1, 7)):
                block = both(p, d, unit(gamma + side * UNIT), UNIT)
                for copy in w_copies(p, d, 2, block, block, place(x, y, (z + step) % 8, k)):
                    copy.start()

    def own_copies(p):
        return [
            pltpu.make_async_copy(a, b, own_sem.at[p, i]) for i, (a, b) in enumerate(zip(both_src(p, 0, D), both(p, 0, 0, D)))
        ]

    def weights_in(p, d):
        @pl.when(d == 0)
        def _():
            for copy in own_copies(p):
                copy.wait()

        @pl.when(d > 0)
        def _():
            w_wait(p, d, 2, 5)

    def t_copy(stage, src, dst, device):
        return pltpu.make_async_remote_copy(
            src_ref=src,
            dst_ref=dst,
            send_sem=t_send.at[stage],
            recv_sem=t_recv.at[stage],
            device_id=device,
            device_id_type=MESH,
        )

    def copies0():
        out = []
        for d in range(1, 8):
            to = (w + d) % 8
            start = (to % 4) * 64 + (to // 4) * 32
            out.append(
                t_copy(0, tok.at[rows(start, 32), :], arrived.at[0, rows(w * 32, 32), :], {"ta": x, "ha": h, "wa": to})
            )
        return out

    def t_total(stage, count):
        block = arrived.at[stage, 0:count, :]
        return t_copy(stage, block, block, partner)

    own_rows = pltpu.make_async_copy(
        tok.at[rows(y * 64 + z_lo * 32, 32), :], arrived.at[0, rows(w * 32, 32), :], own_sem.at[4, 0]
    )

    j = z * 2 + k
    group = z_hi * 4 + k * 2 + z_lo

    def copies1():
        out = []
        for d in range(1, 16):
            to = (j + d) % 16
            to_z, to_k = to // 2, to % 2
            block = (to_z % 2) * 8 + (to_z // 2) * 2 + to_k
            out.append(
                t_copy(
                    1, leaving.at[0, rows(block * 16, 16), :], arrived.at[1, rows(group * 16, 16), :], place(x, y, to_z, to_k)
                )
            )
        return out

    f = x * 4 + y

    def copies2():
        out = []
        for d in range(1, 16):
            to = (f + d) % 16
            to_x, to_y = to // 4, to % 4
            block = ((to_y + phase) % 4) * 4 + to_x
            out.append(
                t_copy(2, leaving.at[1, rows(block * 16, 16), :], arrived.at[2, rows(f * 16, 16), :], place(to_x, to_y, z, k))
            )
        return out

    slot3 = (x % 2) * 8 + z_hi * 2 + k
    to_hi = (y + phase) % 4
    at_home = jnp.logical_and(z_hi == to_hi, k == x // 2)

    def copies3():
        out = []
        for dx in range(4):
            for dy in range(4):
                to_x, to_y = (x + dx) % 4, (y + dy) % 4
                copy = t_copy(
                    3,
                    leaving.at[2, rows((to_x * 4 + to_y) * 16, 16), :],
                    arrived.at[3, rows(slot3 * 16, 16), :],
                    place(to_x, to_y, to_hi * 2 + z_lo, x // 2),
                )
                out.append((dx == 0 and dy == 0, copy))
        return out

    def all_home(act):
        @pl.when(at_home)
        def _():
            act(t_total(3, 240))

        @pl.when(jnp.logical_not(at_home))
        def _():
            act(t_total(3, 256))

    def pair_copy(p, index, src, dst):
        return pltpu.make_async_remote_copy(
            src_ref=src,
            dst_ref=dst,
            send_sem=p_send.at[p, index],
            recv_sem=p_recv.at[p, index],
            device_id=partner,
            device_id_type=MESH,
        )

    def share_copy(p):
        return pair_copy(p, 0, normed.at[p, 0:ROWS, :], normed.at[p, ROWS : 2 * ROWS, :])

    def return_copy(p):
        return pair_copy(p, 1, partial.at[p], partial_in.at[p])

    def greet(stage, peers):
        for peer in peers:
            pl.semaphore_signal(hello.at[stage], inc=1, device_id=peer, device_id_type=MESH)

    lane = lax.broadcasted_iota(jnp.int32, (1, 128), 1)
    left = lane < 64

    def project(p, d):
        tokens = normed[p]
        both_heads = dot(tokens, jnp.concatenate([w_attn[p, d, 0], w_attn[p, d, 1]], axis=1))
        a, b = iotas((256, 256))
        gain = jnp.concatenate([qk_gain[p, 0:1, :] * 0.125] * 2 + [qk_gain[p, 1:2, :]] * 2, axis=1)
        sums = jnp.where(a // 64 == b // 64, 1.0 / 64.0, 0.0).astype(BF16)
        mean = dot((both_heads * both_heads).astype(BF16), sums)
        qkv[:, 0:256] = (both_heads * lax.rsqrt(mean + 1e-6) * gain).astype(BF16)
        qkv[:, 256:384] = dot(tokens, w_attn[p, d, 2]).astype(BF16)

    def attend(d):
        for s in range(2):
            r = slice(s * ROWS, s * ROWS + ROWS)
            queries, key_rows = qkv[r, 0:128], qkv[r, 128:256]
            values = jnp.concatenate([qkv[r, 256:384], jnp.ones((ROWS, 128), BF16)], axis=1)
            results = []
            for side in range(2):
                mine = jnp.where(left if side == 0 else jnp.logical_not(left), queries, jnp.zeros_like(queries))
                weights = jnp.exp(dot_t(mine, key_rows)).astype(BF16) * mask[...]
                summed = dot(weights, values)
                results.append(summed[:, :128] / summed[:, 128:])
            heads[r, rows(d * 128, 128)] = jnp.where(left, results[0], results[1]).astype(BF16)

    def quarters(relays, work):
        def step(i, carry):
            work(i + i // 2 - 2 * (i // 3))
            for at, relay in relays:
                pl.when(i == at)(relay)
            return carry

        lax.fori_loop(0, 4, step, 0)

    def attention(p, *relays):
        def work(d):
            weights_in(p, d)
            project(p, d)
            attend(d)

        quarters(relays, work)
        finish(p, heads, w_out[p])

    def mlp_quarter(d):
        weights_in(3, d)
        tokens = normed[3]
        gate = dot(tokens, w_in[d, 0])
        up = dot(tokens, w_in[d, 1])
        hidden[:, rows(d * 256, 256)] = (gate / (1.0 + jnp.exp(-gate)) * up).astype(BF16)

    def finish(p, left_ref, right_ref):
        partial[p] = dot(left_ref[ROWS:, :], right_ref).astype(BF16)
        return_copy(p).start()
        stream[...] = stream[...] + dot(left_ref[:ROWS, :], right_ref)
        return_copy(p).wait_recv()
        stream[...] = stream[...] + partial_in[p].astype(F32)

    def begin(p):
        normed[p, 0:ROWS, :] = rms(stream[...], norm_gain[p : p + 1, :]).astype(BF16)
        share_copy(p).start()

    for p in range(4):
        for copy in own_copies(p):
            copy.start()
    own_rows.start()
    barrier = pltpu.get_barrier_semaphore()
    greeted = [place((x + e) % 4, y, z, k) for e in (1, 2, 3)]
    greeted += [{"ta": x, "ha": h, "wa": (w + d) % 8} for d in range(1, 8)]
    greeted += [partner, place(x, y, (z + 7 + 2 * z_lo) % 8, k)]
    for peer in greeted:
        pl.semaphore_signal(barrier, inc=1, device_id=peer, device_id_type=MESH)
    pl.semaphore_wait(barrier, len(greeted))
    for copy in copies0():
        copy.start()
    for p in range(2):
        for kind in range(2):
            x_send(p, kind)
    greet(0, [place(x, y, (z + 1) % 8, k), place(x, y, (z + 7) % 8, k)])

    a, b = iotas((ROWS, ROWS))
    mask[...] = jnp.where((a // 8) % 4 == (b // 8) % 4, 1.0, 0.0).astype(BF16)
    pl.semaphore_wait(hello.at[0], 2)
    greet(1, [place(x, y, (z + 2) % 8, k), place(x, y, (z + 6) % 8, k)])
    forward_y(0, 1, 3)
    own_rows.wait()
    t_total(0, 224).wait_recv()
    stream[...] = arrived[0].astype(F32)
    begin(0)
    forward_y(0, 2)
    pl.semaphore_wait(hello.at[1], 2)
    greet(2, [partner])
    share_copy(0).wait_recv()

    def late():
        x_send(2, 0)
        x_send(2, 1)
        forward_y(1, 1, 3)

    attention(0, (0, lambda: forward_z(0, 1, 3)), (1, lambda: forward_z(0, 2)), (2, late))
    pl.semaphore_wait(hello.at[2], 1)

    order = one_hot(lambda o: ((o // 128) * 4 + o % 4) * 32 + ((o // 4) % 4) * 8 + (o // 16) % 8)
    leaving[0] = dot(order, stream[...].astype(BF16)).astype(BF16)
    for copy in copies1():
        copy.start()
    x_send(3, 0)
    own_block = z_lo * 8 + z_hi * 2 + k
    arrived[1, rows(group * 16, 16), :] = leaving[0, rows(own_block * 16, 16), :]
    a, b = iotas((ROWS, ROWS))
    mask[...] = jnp.where(a % 4 == b % 4, 1.0, 0.0).astype(BF16)
    forward_y(1, 2)
    forward_z(1, 1, 3, 2)
    t_total(1, 240).wait_recv()
    stream[...] = arrived[1].astype(F32)
    begin(1)
    forward_y(2, 1, 3)
    share_copy(1).wait_recv()
    attention(1, (0, lambda: forward_y(2, 2)), (2, lambda: forward_z(2, 1, 3)))

    leaving[1] = stream[...].astype(BF16)
    for copy in copies2():
        copy.start()
    x_send(3, 1, (1, 3))
    arrived[2, rows(f * 16, 16), :] = leaving[1, rows((((y + phase) % 4) * 4 + x) * 16, 16), :]
    a, b = iotas((ROWS, ROWS))
    mask[...] = jnp.where(jnp.logical_and(a % 16 == b % 16, b // 16 <= a // 16), 1.0, 0.0).astype(BF16)
    forward_z(2, 2)
    forward_y(3, 1, 3, 2)
    t_total(2, 240).wait_recv()
    x_send(3, 1, (2,))
    stream[...] = arrived[2].astype(F32)
    begin(2)
    share_copy(2).wait_recv()
    attention(2, (0, lambda: forward_z(3, 1)), (1, lambda: forward_z(3, 3)))

    begin(3)
    share_copy(3).wait_recv()
    quarters(((1, lambda: forward_z(3, 2)),), mlp_quarter)
    finish(3, hidden, w_down[...])

    order = one_hot(lambda o: ((o // 64) * 4 + (o // 4) % 4) * 16 + (o % 4) * 4 + (o // 16) % 4)
    leaving[2] = dot(order, stream[...].astype(BF16)).astype(BF16)
    for maybe_self, copy in copies3():
        if maybe_self:

            @pl.when(jnp.logical_not(at_home))
            def _():
                copy.start()

            @pl.when(at_home)
            def _():
                arrived[3, rows(slot3 * 16, 16), :] = leaving[2, rows(f * 16, 16), :]

        else:
            copy.start()
    all_home(lambda copy: copy.wait_recv())
    order = one_hot(lambda o: (((o // 32) % 2) * 8 + o % 8) * 16 + (o // 64) * 4 + (o // 8) % 4)
    out_ref[...] = dot(order, arrived[3]).astype(BF16)

    t_total(0, 224).wait_send()
    t_total(1, 240).wait_send()
    t_total(2, 240).wait_send()
    all_home(lambda copy: copy.wait_send())
    for p in range(4):
        for _ in range(3):
            w_total(p, 0, 0, 8).wait_send()
        share_copy(p).wait_send()
        return_copy(p).wait_send()


def local(tokens, norm_gain, qkv_weight, qk_gain, out_weight, ffn_in, ffn_out):
    qkv_src = qkv_weight.transpose(0, 2, 1, 3)
    in_src = ffn_in.transpose(1, 0, 2)
    vmem, hbm = pl.BlockSpec(memory_space=pltpu.VMEM), pl.BlockSpec(memory_space=pl.ANY)
    result = pl.pallas_call(
        kernel,
        out_shape=jax.ShapeDtypeStruct((ROWS, D), BF16),
        in_specs=[hbm, hbm, hbm, hbm, hbm, vmem, vmem],
        out_specs=vmem,
        scratch_shapes=[
            pltpu.VMEM((3, 4, 3, D, 128), BF16),
            pltpu.VMEM((3, 512, D), BF16),
            pltpu.VMEM((4, 2, D, 256), BF16),
            pltpu.VMEM((D, D), BF16),
            pltpu.VMEM((4, ROWS, D), BF16),
            pltpu.VMEM((3, ROWS, D), BF16),
            pltpu.VMEM((ROWS, D), F32),
            pltpu.VMEM((4, 2 * ROWS, D), BF16),
            pltpu.VMEM((4, ROWS, D), BF16),
            pltpu.VMEM((4, ROWS, D), BF16),
            pltpu.VMEM((2 * ROWS, 384), BF16),
            pltpu.VMEM((2 * ROWS, 512), BF16),
            pltpu.VMEM((2 * ROWS, D), BF16),
            pltpu.VMEM((ROWS, ROWS), BF16),
            pltpu.SemaphoreType.DMA((4,)),
            pltpu.SemaphoreType.DMA((4, 4, 3)),
            pltpu.SemaphoreType.DMA((5, 2)),
            pltpu.SemaphoreType.DMA((4,)),
            pltpu.SemaphoreType.DMA((4,)),
            pltpu.SemaphoreType.DMA((4, 2)),
            pltpu.SemaphoreType.DMA((4, 2)),
            pltpu.SemaphoreType.REGULAR((3,)),
        ],
        compiler_params=pltpu.CompilerParams(collective_id=0, has_side_effects=True, vmem_limit_bytes=60 * 2**20),
    )(tokens.reshape(ROWS, D), qkv_src, out_weight, in_src, ffn_out, norm_gain, qk_gain)
    return result.reshape(tokens.shape)


def solution(mesh):
    return jax.shard_map(
        local,
        mesh=mesh,
        in_specs=(
            P(None, "ta", "ha", "wa", None),
            P(),
            P(None, None, None, "ta"),
            P(),
            P(None, "ta", None),
            P(None, None, "ta"),
            P("ta", None),
        ),
        out_specs=P(None, "ta", "ha", "wa", None),
        check_vma=False,
    )
```

time: 200 us -> 143 us (0.71); the launches traced: 197 us -> 143 us
  Pallas kernels: 178 us -> 138 us
  local copies, waits for them, and re-layouts: 13.3 us -> 5.14 us
  other arithmetic: 5.99 us -> 0 us
    pallas_call x1, Pallas kernels: 178 us -> 138 us  [local(): pl.pallas_call(kernel, out_shape=jax.ShapeDtypeStruct((ROWS, D), BF16), i...]
    concatenate x2 -> x0, other arithmetic: 5.92 us -> none  [the longest x1 3.59 us: local(): attn_src = jnp.concatenate([qkv_half, out_half[:, None]], axis=1)]
    dynamic_slice x3 -> x0, local copies, waits for them, and re-layouts: 3.54 us -> none  [the longest x1 1.87 us: local(): down_half = lax.dynamic_slice_in_dim(ffn_out, k * 256, 256, 0).T]
    transpose x1 -> x0, local copies, waits for them, and re-layouts: 3.41 us -> none  [local(): lax.dynamic_slice_in_dim(qkv_weight, k * 128, 128, 3).transpose(0, 2, 1, 3)]
    unnamed x12 -> x2, local copies, waits for them, and re-layouts: 5.62 us -> 5.14 us
where the time goes in v1:
time: 143 us
  Pallas kernels  138 us (97%)
  local copies, waits for them, and re-layouts  5.14 us (4%)
    pallas_call x1, Pallas kernels, local(): pl.pallas_call(kernel, out_shape=jax.ShapeDtypeStruct((ROWS, D), BF16), i...  138 us
    unnamed x2, local copies, waits for them, and re-layouts  5.14 us

profile of v1, /device:TPU:6, one launch (start us, length us, event | category | flops | bytes accessed | tf_op | source)
XLA Modules:
  0.0 143.0 jit_solution(3370266936847031879)
XLA Ops:
  0.0 3.3 %copy.10 = bf16[1024,2,512]{2,0,1:T(8,128)(2,1)} copy(bf16[1024,2,512]{2,1,0:T(2,128)(2,1)} %param.12) | data formatting | bytes 4194304 | tf_op args[5]
  3.3 137.9 %shard_map.73 = bf16[256,1024]{1,0:T(8,128)(2,1)} custom-call(bf16[256,1024]{1,0:T(8,128)(2,1)} %bitcast.9, bf16[3,3,1024,256]{3,2,1,0:T(8,128)(2,1)} %bitcast.7, bf16[3,256,1024]{2,1,0:T(8,128)(2,1)} %out_src.1, bf16[2,1024,512]{2,1,0:T(8,128)(2,1)} %bitcast.6, bf16[512,1024]{1,0:T(8,128)(2,1)} %down_src.1, f32[4,1024]{1,0:T(4,128)} %norm_gain.1, ...), custom_call_target="tpu_custom_call" | custom-call | tf_op jit(solution)/shard_map/pallas_call | solution.py:444
  141.2 1.9 %copy.12 = bf16[1,4,8,8,1024]{4,3,2,1,0:T(8,128)(2,1)} copy(bf16[1,4,8,8,1024]{4,3,2,1,0:T(8,128)(2,1)} %bitcast.8) | data formatting | bytes 1048576

commit v2 on v1

--- a/solution.py
+++ b/solution.py
@@ -80,7 +80,6 @@
     w = lax.axis_index("wa")
     z_hi, k, z_lo, y = h // 2, h % 2, w // 4, w % 4
     z = z_hi * 2 + z_lo
-    phase = z_hi + 2 * z_lo + k
     partner = place(x, y, z, 1 - k)
 
     def both(p, d, start, size):
@@ -124,43 +123,50 @@
 
     gamma = pl.multiple_of(512 + z_lo * 256, 256)
 
-    def x_send(p, kind, steps=(1, 3, 2)):
-        for e in steps:
-            peer = place((x + e) % 4, y, z, k)
+    def start_all(copies):
+        for copy in copies:
+            copy.start()
+
+    def x_send(p, kind):
+        for e in (1, 3):
             start, size = ((unit(y * UNIT), UNIT), (gamma, 256))[kind]
-            for copy in w_copies(p, 4 - e, kind, both_src(p, start, size), both(p, 4 - e, start, size), peer):
-                copy.start()
+            start_all(
+                w_copies(p, 4 - e, kind, both_src(p, start, size), both(p, 4 - e, start, size), place((x + e) % 4, y, z, k))
+            )
+
+    def x_relay(p, d, kind, start):
+        block, there = both(p, d, start, UNIT), both(p, 2, start, UNIT)
+        start_all(w_copies(p, 2, kind, block, there, place((x + 4 - d) % 4, y, z, k)))
 
     def forward_y(p, *quarters):
         for d in quarters:
             w_wait(p, d, 0, 1)
             block = both(p, d, unit(y * UNIT), UNIT)
+            if d != 2:
+                pl.when(k == (0 if d == 3 else 1))(lambda: x_relay(p, d, 0, unit(y * UNIT)))
             for e in (1, 3, 2):
-                for copy in w_copies(p, d, 2, block, block, place(x, (y + e) % 4, z, k)):
-                    copy.start()
+                start_all(w_copies(p, d, 2, block, block, place(x, (y + e) % 4, z, k)))
 
     def forward_z(p, *quarters):
         for d in quarters:
             w_wait(p, d, 1, 2)
+            if d != 2:
+                x_relay(p, d, 1, unit(gamma if d == 3 else gamma + UNIT))
             for side, step in ((0, 1), (1, 7)):
                 block = both(p, d, unit(gamma + side * UNIT), UNIT)
-                for copy in w_copies(p, d, 2, block, block, place(x, y, (z + step) % 8, k)):
-                    copy.start()
+                start_all(w_copies(p, d, 2, block, block, place(x, y, (z + step) % 8, k)))
 
     def own_copies(p):
         return [
             pltpu.make_async_copy(a, b, own_sem.at[p, i]) for i, (a, b) in enumerate(zip(both_src(p, 0, D), both(p, 0, 0, D)))
         ]
 
+    def own_in(p):
+        for copy in own_copies(p):
+            copy.wait()
+
     def weights_in(p, d):
-        @pl.when(d == 0)
-        def _():
-            for copy in own_copies(p):
-                copy.wait()
-
-        @pl.when(d > 0)
-        def _():
-            w_wait(p, d, 2, 5)
+        w_wait(p, d, 2, 5)
 
     def t_copy(stage, src, dst, device):
         return pltpu.make_async_remote_copy(
@@ -208,19 +214,31 @@
 
     f = x * 4 + y
 
+    def turn(to_y):
+        return (to_y + 2 * z_lo + k) % 4
+
+    def moved(c, to_x):
+        half_way = jnp.where(c == 2, jnp.where(to_x // 2 == 0, 1, 3), jnp.where(to_x % 2 == 0, c, 0))
+        return jnp.where(c == 0, 0, half_way)
+
     def copies2():
         out = []
-        for d in range(1, 16):
+        for d in range(16):
             to = (f + d) % 16
             to_x, to_y = to // 4, to % 4
-            block = ((to_y + phase) % 4) * 4 + to_x
-            out.append(
-                t_copy(2, leaving.at[1, rows(block * 16, 16), :], arrived.at[2, rows(f * 16, 16), :], place(to_x, to_y, z, k))
-            )
+            c = turn(to_y)
+            block = ((z_hi + c) % 4) * 4 + to_x
+            to_z = ((z_hi + moved(c, to_x)) % 4) * 2 + z_lo
+            copy = t_copy(2, leaving.at[1, rows(block * 16, 16), :], arrived.at[2, rows(f * 16, 16), :], place(to_x, to_y, to_z, k))
+            out.append((d == 0, copy))
         return out
 
-    slot3 = (x % 2) * 8 + z_hi * 2 + k
-    to_hi = (y + phase) % 4
+    my_turn = turn(y)
+    stays = moved(my_turn, x) == 0
+    from_hi = (z_hi + 4 - moved(my_turn, x)) % 4
+
+    slot3 = (x % 2) * 8 + from_hi * 2 + k
+    to_hi = (from_hi + my_turn) % 4
     at_home = jnp.logical_and(z_hi == to_hi, k == x // 2)
 
     def copies3():
@@ -237,14 +255,17 @@
                 out.append((dx == 0 and dy == 0, copy))
         return out
 
-    def all_home(act):
-        @pl.when(at_home)
-        def _():
-            act(t_total(3, 240))
-
-        @pl.when(jnp.logical_not(at_home))
-        def _():
-            act(t_total(3, 256))
+    def unless(kept, stage, act):
+        pl.when(kept)(lambda: act(t_total(stage, 240)))
+        pl.when(jnp.logical_not(kept))(lambda: act(t_total(stage, 256)))
+
+    def send_all(copies, kept, keep):
+        for maybe_self, copy in copies:
+            if maybe_self:
+                pl.when(jnp.logical_not(kept))(copy.start)
+                pl.when(kept)(keep)
+            else:
+                copy.start()
 
     def pair_copy(p, index, src, dst):
         return pltpu.make_async_remote_copy(
@@ -269,58 +290,77 @@
     lane = lax.broadcasted_iota(jnp.int32, (1, 128), 1)
     left = lane < 64
 
-    def project(p, d):
-        tokens = normed[p]
+    own, other, all_rows = slice(0, ROWS), slice(ROWS, 2 * ROWS), slice(0, 2 * ROWS)
+
+    def project(p, d, r):
+        tokens = normed[p, r, :]
         both_heads = dot(tokens, jnp.concatenate([w_attn[p, d, 0], w_attn[p, d, 1]], axis=1))
         a, b = iotas((256, 256))
         gain = jnp.concatenate([qk_gain[p, 0:1, :] * 0.125] * 2 + [qk_gain[p, 1:2, :]] * 2, axis=1)
         sums = jnp.where(a // 64 == b // 64, 1.0 / 64.0, 0.0).astype(BF16)
         mean = dot((both_heads * both_heads).astype(BF16), sums)
-        qkv[:, 0:256] = (both_heads * lax.rsqrt(mean + 1e-6) * gain).astype(BF16)
-        qkv[:, 256:384] = dot(tokens, w_attn[p, d, 2]).astype(BF16)
-
-    def attend(d):
-        for s in range(2):
-            r = slice(s * ROWS, s * ROWS + ROWS)
-            queries, key_rows = qkv[r, 0:128], qkv[r, 128:256]
-            values = jnp.concatenate([qkv[r, 256:384], jnp.ones((ROWS, 128), BF16)], axis=1)
-            results = []
-            for side in range(2):
-                mine = jnp.where(left if side == 0 else jnp.logical_not(left), queries, jnp.zeros_like(queries))
-                weights = jnp.exp(dot_t(mine, key_rows)).astype(BF16) * mask[...]
-                summed = dot(weights, values)
-                results.append(summed[:, :128] / summed[:, 128:])
-            heads[r, rows(d * 128, 128)] = jnp.where(left, results[0], results[1]).astype(BF16)
-
-    def quarters(relays, work):
-        def step(i, carry):
-            work(i + i // 2 - 2 * (i // 3))
-            for at, relay in relays:
-                pl.when(i == at)(relay)
-            return carry
-
-        lax.fori_loop(0, 4, step, 0)
-
-    def attention(p, *relays):
-        def work(d):
+        qkv[r, 256:384] = dot(tokens, w_attn[p, d, 2]).astype(BF16)
+        qkv[r, 0:256] = (both_heads * lax.rsqrt(mean + 1e-6) * gain).astype(BF16)
+
+    def attend(d, r):
+        queries, key_rows = qkv[r, 0:128], qkv[r, 128:256]
+        values = jnp.concatenate([qkv[r, 256:384], jnp.ones((ROWS, 128), BF16)], axis=1)
+        results = []
+        for side in range(2):
+            mine = jnp.where(left if side == 0 else jnp.logical_not(left), queries, jnp.zeros_like(queries))
+            weights = jnp.exp(dot_t(mine, key_rows)).astype(BF16) * mask[...]
+            summed = dot(weights, values)
+            results.append(summed[:, :128] / summed[:, 128:])
+        heads[r, d * 128 : d * 128 + 128] = jnp.where(left, results[0], results[1]).astype(BF16)
+
+    def attention(p, relay0=None, relay1=None, relay3=None):
+        own_in(p)
+        project(p, 0, own)
+        attend(0, own)
+        share_copy(p).wait_recv()
+        project(p, 0, other)
+        attend(0, other)
+        for relay, d in ((relay0, 1), (relay1, 3)):
+            if relay is not None:
+                relay()
             weights_in(p, d)
-            project(p, d)
-            attend(d)
-
-        quarters(relays, work)
+            project(p, d, all_rows)
+            attend(d, own)
+            attend(d, other)
+        if relay3 is not None:
+            relay3()
+        weights_in(p, 2)
+        project(p, 2, other)
+        attend(2, other)
+        partial[p] = dot(heads[other, :], w_out[p]).astype(BF16)
+        return_copy(p).start()
+        project(p, 2, own)
+        attend(2, own)
         finish(p, heads, w_out[p])
 
-    def mlp_quarter(d):
-        weights_in(3, d)
-        tokens = normed[3]
+    def mlp_quarter(d, r):
+        tokens = normed[3, r, :]
         gate = dot(tokens, w_in[d, 0])
         up = dot(tokens, w_in[d, 1])
-        hidden[:, rows(d * 256, 256)] = (gate / (1.0 + jnp.exp(-gate)) * up).astype(BF16)
+        hidden[r, d * 256 : d * 256 + 256] = (gate / (1.0 + jnp.exp(-gate)) * up).astype(BF16)
+
+    def mlp():
+        own_in(3)
+        mlp_quarter(0, own)
+        share_copy(3).wait_recv()
+        mlp_quarter(0, other)
+        for d in (1, 3):
+            weights_in(3, d)
+            mlp_quarter(d, all_rows)
+        weights_in(3, 2)
+        mlp_quarter(2, other)
+        partial[3] = dot(hidden[other, :], w_down[...]).astype(BF16)
+        return_copy(3).start()
+        mlp_quarter(2, own)
+        finish(3, hidden, w_down[...])
 
     def finish(p, left_ref, right_ref):
-        partial[p] = dot(left_ref[ROWS:, :], right_ref).astype(BF16)
-        return_copy(p).start()
-        stream[...] = stream[...] + dot(left_ref[:ROWS, :], right_ref)
+        stream[...] = stream[...] + dot(left_ref[own, :], right_ref)
         return_copy(p).wait_recv()
         stream[...] = stream[...] + partial_in[p].astype(F32)
 
@@ -339,11 +379,9 @@
     for peer in greeted:
         pl.semaphore_signal(barrier, inc=1, device_id=peer, device_id_type=MESH)
     pl.semaphore_wait(barrier, len(greeted))
-    for copy in copies0():
-        copy.start()
-    for p in range(2):
-        for kind in range(2):
-            x_send(p, kind)
+    start_all(copies0())
+    x_send(0, 0)
+    x_send(0, 1)
     greet(0, [place(x, y, (z + 1) % 8, k), place(x, y, (z + 7) % 8, k)])
 
     a, b = iotas((ROWS, ROWS))
@@ -351,85 +389,83 @@
     pl.semaphore_wait(hello.at[0], 2)
     greet(1, [place(x, y, (z + 2) % 8, k), place(x, y, (z + 6) % 8, k)])
     forward_y(0, 1, 3)
+    x_send(1, 0)
     own_rows.wait()
     t_total(0, 224).wait_recv()
     stream[...] = arrived[0].astype(F32)
     begin(0)
-    forward_y(0, 2)
     pl.semaphore_wait(hello.at[1], 2)
     greet(2, [partner])
-    share_copy(0).wait_recv()
-
-    def late():
+
+    def relays00():
+        forward_z(0, 1, 3)
+        x_send(1, 1)
+        forward_y(0, 2)
+
+    def relays01():
+        forward_z(0, 2)
+        forward_y(1, 1, 3)
         x_send(2, 0)
+
+    def relays02():
+        forward_z(1, 1, 3)
         x_send(2, 1)
-        forward_y(1, 1, 3)
-
-    attention(0, (0, lambda: forward_z(0, 1, 3)), (1, lambda: forward_z(0, 2)), (2, late))
+        forward_y(1, 2)
+
+    attention(0, relays00, relays01, relays02)
     pl.semaphore_wait(hello.at[2], 1)
 
     order = one_hot(lambda o: ((o // 128) * 4 + o % 4) * 32 + ((o // 4) % 4) * 8 + (o // 16) % 8)
     leaving[0] = dot(order, stream[...].astype(BF16)).astype(BF16)
-    for copy in copies1():
-        copy.start()
-    x_send(3, 0)
+    start_all(copies1())
     own_block = z_lo * 8 + z_hi * 2 + k
     arrived[1, rows(group * 16, 16), :] = leaving[0, rows(own_block * 16, 16), :]
     a, b = iotas((ROWS, ROWS))
     mask[...] = jnp.where(a % 4 == b % 4, 1.0, 0.0).astype(BF16)
-    forward_y(1, 2)
-    forward_z(1, 1, 3, 2)
+    forward_z(1, 2)
+    forward_y(2, 1, 3)
+    x_send(3, 0)
     t_total(1, 240).wait_recv()
     stream[...] = arrived[1].astype(F32)
     begin(1)
-    forward_y(2, 1, 3)
-    share_copy(1).wait_recv()
-    attention(1, (0, lambda: forward_y(2, 2)), (2, lambda: forward_z(2, 1, 3)))
+    forward_z(2, 1, 3)
+    x_send(3, 1)
+    forward_y(2, 2)
+
+    attention(1, None, lambda: forward_z(2, 2), lambda: forward_y(3, 1))
 
     leaving[1] = stream[...].astype(BF16)
-    for copy in copies2():
-        copy.start()
-    x_send(3, 1, (1, 3))
-    arrived[2, rows(f * 16, 16), :] = leaving[1, rows((((y + phase) % 4) * 4 + x) * 16, 16), :]
+
+    def keep2():
+        arrived[2, rows(f * 16, 16), :] = leaving[1, rows((((z_hi + my_turn) % 4) * 4 + x) * 16, 16), :]
+
+    send_all(copies2(), stays, keep2)
     a, b = iotas((ROWS, ROWS))
     mask[...] = jnp.where(jnp.logical_and(a % 16 == b % 16, b // 16 <= a // 16), 1.0, 0.0).astype(BF16)
-    forward_z(2, 2)
-    forward_y(3, 1, 3, 2)
-    t_total(2, 240).wait_recv()
-    x_send(3, 1, (2,))
+    unless(stays, 2, lambda copy: copy.wait_recv())
+    forward_z(3, 1, 3)
+    forward_y(3, 3)
     stream[...] = arrived[2].astype(F32)
     begin(2)
-    share_copy(2).wait_recv()
-    attention(2, (0, lambda: forward_z(3, 1)), (1, lambda: forward_z(3, 3)))
+    attention(2, lambda: forward_y(3, 2), lambda: forward_z(3, 2))
 
     begin(3)
-    share_copy(3).wait_recv()
-    quarters(((1, lambda: forward_z(3, 2)),), mlp_quarter)
-    finish(3, hidden, w_down[...])
+    mlp()
 
     order = one_hot(lambda o: ((o // 64) * 4 + (o // 4) % 4) * 16 + (o % 4) * 4 + (o // 16) % 4)
     leaving[2] = dot(order, stream[...].astype(BF16)).astype(BF16)
-    for maybe_self, copy in copies3():
-        if maybe_self:
-
-            @pl.when(jnp.logical_not(at_home))
-            def _():
-                copy.start()
-
-            @pl.when(at_home)
-            def _():
-                arrived[3, rows(slot3 * 16, 16), :] = leaving[2, rows(f * 16, 16), :]
-
-        else:
-            copy.start()
-    all_home(lambda copy: copy.wait_recv())
+    def keep3():
+        arrived[3, rows(slot3 * 16, 16), :] = leaving[2, rows(f * 16, 16), :]
+
+    send_all(copies3(), at_home, keep3)
+    unless(at_home, 3, lambda copy: copy.wait_recv())
     order = one_hot(lambda o: (((o // 32) % 2) * 8 + o % 8) * 16 + (o // 64) * 4 + (o // 8) % 4)
     out_ref[...] = dot(order, arrived[3]).astype(BF16)
 
     t_total(0, 224).wait_send()
     t_total(1, 240).wait_send()
-    t_total(2, 240).wait_send()
-    all_home(lambda copy: copy.wait_send())
+    unless(stays, 2, lambda copy: copy.wait_send())
+    unless(at_home, 3, lambda copy: copy.wait_send())
     for p in range(4):
         for _ in range(3):
             w_total(p, 0, 0, 8).wait_send()

time: 143 us -> 125 us (0.87); the launches traced: 143 us -> 123 us
  Pallas kernels: 138 us -> 118 us
    pallas_call x1, Pallas kernels: 138 us -> 118 us  [local(): pl.pallas_call(kernel, out_shape=jax.ShapeDtypeStruct((ROWS, D), BF16), i...]
where the time goes in v2:
time: 125 us; the launch traced here: 123 us
  Pallas kernels  118 us (94%)
  local copies, waits for them, and re-layouts  5.14 us (4%)
    pallas_call x1, Pallas kernels, local(): pl.pallas_call(kernel, out_shape=jax.ShapeDtypeStruct((ROWS, D), BF16), i...  118 us
    unnamed x2, local copies, waits for them, and re-layouts  5.14 us

profile of v2, /device:TPU:6, one launch (start us, length us, event | category | flops | bytes accessed | tf_op | source)
XLA Modules:
  0.0 123.2 jit_solution(18155468315054483937)
XLA Ops:
  0.0 3.3 %copy.10 = bf16[1024,2,512]{2,0,1:T(8,128)(2,1)} copy(bf16[1024,2,512]{2,1,0:T(2,128)(2,1)} %param.12) | data formatting | bytes 4194304 | tf_op args[5]
  3.3 118.0 %shard_map.73 = bf16[256,1024]{1,0:T(8,128)(2,1)} custom-call(bf16[256,1024]{1,0:T(8,128)(2,1)} %bitcast.9, bf16[3,3,1024,256]{3,2,1,0:T(8,128)(2,1)} %bitcast.7, bf16[3,256,1024]{2,1,0:T(8,128)(2,1)} %out_src.1, bf16[2,1024,512]{2,1,0:T(8,128)(2,1)} %bitcast.6, bf16[512,1024]{1,0:T(8,128)(2,1)} %down_src.1, f32[4,1024]{1,0:T(4,128)} %norm_gain.1, ...), custom_call_target="tpu_custom_call" | custom-call | tf_op jit(solution)/shard_map/pallas_call | solution.py:480
  121.3 1.9 %copy.12 = bf16[1,4,8,8,1024]{4,3,2,1,0:T(8,128)(2,1)} copy(bf16[1,4,8,8,1024]{4,3,2,1,0:T(8,128)(2,1)} %bitcast.8) | data formatting | bytes 1048576

commit v3 on v2

--- a/solution.py
+++ b/solution.py
@@ -66,6 +66,7 @@
     heads,
     hidden,
     mask,
+    raw,
     w_send,
     w_recv,
     own_sem,
@@ -94,7 +95,7 @@
                 out_src.at[p, rows(k * 128, 128), pl.ds(start, size)],
             )
         return (
-            in_src.at[:, pl.ds(start, size), rows(k * 256, 256)],
+            w_in.at[0, :, pl.ds(start, size), :],
             down_src.at[rows(k * 256, 256), pl.ds(start, size)],
         )
 
@@ -144,8 +145,20 @@
             block = both(p, d, unit(y * UNIT), UNIT)
             if d != 2:
                 pl.when(k == (0 if d == 3 else 1))(lambda: x_relay(p, d, 0, unit(y * UNIT)))
-            for e in (1, 3, 2):
-                start_all(w_copies(p, d, 2, block, block, place(x, (y + e) % 4, z, k)))
+            for e, kind in ((1, 3), (3, 4)):
+                start_all(w_copies(p, d, kind, block, block, place(x, (y + e) % 4, z, k)))
+
+    def relay_y(p, *quarters):
+        for d in quarters:
+            for kind in (3, 4):
+                w_wait(p, d, kind, 1)
+            for core, at, to in ((0, (y + 3) % 4, (y + 1) % 4), (1, (y + 1) % 4, (y + 3) % 4)):
+
+                def send(at=at, to=to):
+                    block = both(p, d, unit(at * UNIT), UNIT)
+                    start_all(w_copies(p, d, 2, block, block, place(x, to, z, k)))
+
+                pl.when(k == core)(send)
 
     def forward_z(p, *quarters):
         for d in quarters:
@@ -156,17 +169,27 @@
                 block = both(p, d, unit(gamma + side * UNIT), UNIT)
                 start_all(w_copies(p, d, 2, block, block, place(x, y, (z + step) % 8, k)))
 
-    def own_copies(p):
-        return [
-            pltpu.make_async_copy(a, b, own_sem.at[p, i]) for i, (a, b) in enumerate(zip(both_src(p, 0, D), both(p, 0, 0, D)))
-        ]
+    def own_copy(p, i):
+        src, dst = (both_src(p, 0, D)[i], both(p, 0, 0, D)[i]) if (p, i) != (3, 0) else (in_src.at[:, :, rows(k * 256, 256)], raw)
+        return pltpu.make_async_copy(src, dst, own_sem.at[p, i])
+
+    def split_in():
+        own_copy(3, 0).wait()
+        out, into = iotas((2 * UNIT, 2 * UNIT))
+        pick = jnp.where(into == 2 * (out % UNIT) + out // UNIT, 1.0, 0.0).astype(BF16)
+        for block in range(D // UNIT):
+            r = slice(block * UNIT, block * UNIT + UNIT)
+            apart = dot(pick, raw[r].reshape(2 * UNIT, 256)).astype(BF16)
+            w_in[0, 0, r, :] = apart[:UNIT]
+            w_in[0, 1, r, :] = apart[UNIT:]
 
     def own_in(p):
-        for copy in own_copies(p):
-            copy.wait()
+        if p < 3:
+            own_copy(p, 0).wait()
+        own_copy(p, 1).wait()
 
     def weights_in(p, d):
-        w_wait(p, d, 2, 5)
+        w_wait(p, d, 2, 3)
 
     def t_copy(stage, src, dst, device):
         return pltpu.make_async_remote_copy(
@@ -369,8 +392,8 @@
         share_copy(p).start()
 
     for p in range(4):
-        for copy in own_copies(p):
-            copy.start()
+        own_copy(p, 0).start()
+        own_copy(p, 1).start()
     own_rows.start()
     barrier = pltpu.get_barrier_semaphore()
     greeted = [place((x + e) % 4, y, z, k) for e in (1, 2, 3)]
@@ -400,17 +423,20 @@
     def relays00():
         forward_z(0, 1, 3)
         x_send(1, 1)
+        relay_y(0, 1)
         forward_y(0, 2)
+        relay_y(0, 3)
+        split_in()
 
     def relays01():
         forward_z(0, 2)
+        relay_y(0, 2)
         forward_y(1, 1, 3)
         x_send(2, 0)
 
     def relays02():
         forward_z(1, 1, 3)
         x_send(2, 1)
-        forward_y(1, 2)
 
     attention(0, relays00, relays01, relays02)
     pl.semaphore_wait(hello.at[2], 1)
@@ -422,17 +448,25 @@
     arrived[1, rows(group * 16, 16), :] = leaving[0, rows(own_block * 16, 16), :]
     a, b = iotas((ROWS, ROWS))
     mask[...] = jnp.where(a % 4 == b % 4, 1.0, 0.0).astype(BF16)
+    relay_y(1, 1, 3)
+    forward_y(1, 2)
     forward_z(1, 2)
     forward_y(2, 1, 3)
     x_send(3, 0)
+    relay_y(1, 2)
     t_total(1, 240).wait_recv()
     stream[...] = arrived[1].astype(F32)
     begin(1)
     forward_z(2, 1, 3)
     x_send(3, 1)
+    relay_y(2, 1, 3)
     forward_y(2, 2)
 
-    attention(1, None, lambda: forward_z(2, 2), lambda: forward_y(3, 1))
+    def relays12():
+        forward_y(3, 1, 3)
+        forward_z(2, 2)
+
+    attention(1, None, None, relays12)
 
     leaving[1] = stream[...].astype(BF16)
 
@@ -442,12 +476,19 @@
     send_all(copies2(), stays, keep2)
     a, b = iotas((ROWS, ROWS))
     mask[...] = jnp.where(jnp.logical_and(a % 16 == b % 16, b // 16 <= a // 16), 1.0, 0.0).astype(BF16)
+    relay_y(2, 2)
     unless(stays, 2, lambda copy: copy.wait_recv())
+    forward_y(3, 2)
     forward_z(3, 1, 3)
-    forward_y(3, 3)
+    relay_y(3, 1, 3)
     stream[...] = arrived[2].astype(F32)
     begin(2)
-    attention(2, lambda: forward_y(3, 2), lambda: forward_z(3, 2))
+
+    def relays21():
+        forward_z(3, 2)
+        relay_y(3, 2)
+
+    attention(2, None, None, relays21)
 
     begin(3)
     mlp()
@@ -475,7 +516,6 @@
 
 def local(tokens, norm_gain, qkv_weight, qk_gain, out_weight, ffn_in, ffn_out):
     qkv_src = qkv_weight.transpose(0, 2, 1, 3)
-    in_src = ffn_in.transpose(1, 0, 2)
     vmem, hbm = pl.BlockSpec(memory_space=pltpu.VMEM), pl.BlockSpec(memory_space=pl.ANY)
     result = pl.pallas_call(
         kernel,
@@ -497,8 +537,9 @@
             pltpu.VMEM((2 * ROWS, 512), BF16),
             pltpu.VMEM((2 * ROWS, D), BF16),
             pltpu.VMEM((ROWS, ROWS), BF16),
+            pltpu.VMEM((D, 2, 256), BF16),
             pltpu.SemaphoreType.DMA((4,)),
-            pltpu.SemaphoreType.DMA((4, 4, 3)),
+            pltpu.SemaphoreType.DMA((4, 4, 5)),
             pltpu.SemaphoreType.DMA((5, 2)),
             pltpu.SemaphoreType.DMA((4,)),
             pltpu.SemaphoreType.DMA((4,)),
@@ -507,7 +548,7 @@
             pltpu.SemaphoreType.REGULAR((3,)),
         ],
         compiler_params=pltpu.CompilerParams(collective_id=0, has_side_effects=True, vmem_limit_bytes=60 * 2**20),
-    )(tokens.reshape(ROWS, D), qkv_src, out_weight, in_src, ffn_out, norm_gain, qk_gain)
+    )(tokens.reshape(ROWS, D), qkv_src, out_weight, ffn_in, ffn_out, norm_gain, qk_gain)
     return result.reshape(tokens.shape)
 
 

time: 125 us -> 112 us (0.90)
  Pallas kernels: 118 us -> 108 us
  local copies, waits for them, and re-layouts: 5.14 us -> 1.87 us
    pallas_call x1, Pallas kernels: 118 us -> 108 us  [local(): pl.pallas_call(kernel, out_shape=jax.ShapeDtypeStruct((ROWS, D), BF16), i...]
    unnamed x2 -> x1, local copies, waits for them, and re-layouts: 5.14 us -> 1.87 us
where the time goes in v3:
time: 112 us; the launch traced here: 110 us
  Pallas kernels  108 us (96%)
  local copies, waits for them, and re-layouts  1.87 us (2%)
    pallas_call x1, Pallas kernels, local(): pl.pallas_call(kernel, out_shape=jax.ShapeDtypeStruct((ROWS, D), BF16), i...  108 us

profile of v3, /device:TPU:6, one launch (start us, length us, event | category | flops | bytes accessed | tf_op | source)
XLA Modules:
  0.0 109.5 jit_solution(16300402630911858170)
XLA Ops:
  0.0 107.6 %shard_map.73 = bf16[256,1024]{1,0:T(8,128)(2,1)} custom-call(bf16[256,1024]{1,0:T(8,128)(2,1)} %bitcast.5, bf16[3,3,1024,256]{3,2,1,0:T(8,128)(2,1)} %bitcast.3, bf16[3,256,1024]{2,1,0:T(8,128)(2,1)} %out_src.1, bf16[1024,2,512]{2,1,0:T(2,128)(2,1)} %in_src.1, bf16[512,1024]{1,0:T(8,128)(2,1)} %down_src.1, f32[4,1024]{1,0:T(4,128)} %norm_gain.1, ...), custom_call_target="tpu_custom_call" | custom-call | tf_op jit(solution)/shard_map/pallas_call | solution.py:520
  107.7 1.9 %copy.9 = bf16[1,4,8,8,1024]{4,3,2,1,0:T(8,128)(2,1)} copy(bf16[1,4,8,8,1024]{4,3,2,1,0:T(8,128)(2,1)} %bitcast.4) | data formatting | bytes 1048576

commit v4 on v3

--- a/solution.py
+++ b/solution.py
@@ -67,6 +67,7 @@
     hidden,
     mask,
     raw,
+    tok_in,
     w_send,
     w_recv,
     own_sem,
@@ -85,19 +86,8 @@
 
     def both(p, d, start, size):
         if p < 3:
-            return w_attn.at[p, d, :, pl.ds(start, size), :], w_out.at[p, d * 128 : d * 128 + 128, pl.ds(start, size)]
+            return w_attn.at[p, d, pl.ds(start, size), :], w_out.at[p, d * 128 : d * 128 + 128, pl.ds(start, size)]
         return w_in.at[d, :, pl.ds(start, size), :], w_down.at[d * 256 : d * 256 + 256, pl.ds(start, size)]
-
-    def both_src(p, start, size):
-        if p < 3:
-            return (
-                qkv_src.at[p, :, pl.ds(start, size), rows(k * 128, 128)],
-                out_src.at[p, rows(k * 128, 128), pl.ds(start, size)],
-            )
-        return (
-            w_in.at[0, :, pl.ds(start, size), :],
-            down_src.at[rows(k * 256, 256), pl.ds(start, size)],
-        )
 
     def w_copies(p, d, kind, src, dst, device):
         return [
@@ -132,7 +122,7 @@
         for e in (1, 3):
             start, size = ((unit(y * UNIT), UNIT), (gamma, 256))[kind]
             start_all(
-                w_copies(p, 4 - e, kind, both_src(p, start, size), both(p, 4 - e, start, size), place((x + e) % 4, y, z, k))
+                w_copies(p, 4 - e, kind, both(p, 0, start, size), both(p, 4 - e, start, size), place((x + e) % 4, y, z, k))
             )
 
     def x_relay(p, d, kind, start):
@@ -169,12 +159,16 @@
                 block = both(p, d, unit(gamma + side * UNIT), UNIT)
                 start_all(w_copies(p, d, 2, block, block, place(x, y, (z + step) % 8, k)))
 
-    def own_copy(p, i):
-        src, dst = (both_src(p, 0, D)[i], both(p, 0, 0, D)[i]) if (p, i) != (3, 0) else (in_src.at[:, :, rows(k * 256, 256)], raw)
-        return pltpu.make_async_copy(src, dst, own_sem.at[p, i])
+    def own_copies(p):
+        if p < 3:
+            pairs = [(qkv_src.at[p, t, :, rows(k * 128, 128)], w_attn.at[p, 0, :, t * 128 : t * 128 + 128]) for t in range(3)]
+            pairs.append((out_src.at[p, rows(k * 128, 128), :], w_out.at[p, 0:128, :]))
+        else:
+            pairs = [(in_src.at[:, :, rows(k * 256, 256)], raw), (down_src.at[rows(k * 256, 256), :], w_down.at[0:256, :])]
+        return [pltpu.make_async_copy(a, b, own_sem.at[p, i]) for i, (a, b) in enumerate(pairs)]
 
     def split_in():
-        own_copy(3, 0).wait()
+        own_in(3)
         out, into = iotas((2 * UNIT, 2 * UNIT))
         pick = jnp.where(into == 2 * (out % UNIT) + out // UNIT, 1.0, 0.0).astype(BF16)
         for block in range(D // UNIT):
@@ -184,9 +178,8 @@
             w_in[0, 1, r, :] = apart[UNIT:]
 
     def own_in(p):
-        if p < 3:
-            own_copy(p, 0).wait()
-        own_copy(p, 1).wait()
+        for copy in own_copies(p):
+            copy.wait()
 
     def weights_in(p, d):
         w_wait(p, d, 2, 3)
@@ -207,7 +200,7 @@
             to = (w + d) % 8
             start = (to % 4) * 64 + (to // 4) * 32
             out.append(
-                t_copy(0, tok.at[rows(start, 32), :], arrived.at[0, rows(w * 32, 32), :], {"ta": x, "ha": h, "wa": to})
+                t_copy(0, tok_in.at[rows(start, 32), :], arrived.at[0, rows(w * 32, 32), :], {"ta": x, "ha": h, "wa": to})
             )
         return out
 
@@ -215,14 +208,12 @@
         block = arrived.at[stage, 0:count, :]
         return t_copy(stage, block, block, partner)
 
-    own_rows = pltpu.make_async_copy(
-        tok.at[rows(y * 64 + z_lo * 32, 32), :], arrived.at[0, rows(w * 32, 32), :], own_sem.at[4, 0]
-    )
+    tokens_in = pltpu.make_async_copy(tok, tok_in, own_sem.at[4, 0])
 
     j = z * 2 + k
     group = z_hi * 4 + k * 2 + z_lo
 
-    def copies1():
+    def copies1(cols):
         out = []
         for d in range(1, 16):
             to = (j + d) % 16
@@ -230,7 +221,7 @@
             block = (to_z % 2) * 8 + (to_z // 2) * 2 + to_k
             out.append(
                 t_copy(
-                    1, leaving.at[0, rows(block * 16, 16), :], arrived.at[1, rows(group * 16, 16), :], place(x, y, to_z, to_k)
+                    1, leaving.at[0, rows(block * 16, 16), cols], arrived.at[1, rows(group * 16, 16), cols], place(x, y, to_z, to_k)
                 )
             )
         return out
@@ -244,7 +235,7 @@
         half_way = jnp.where(c == 2, jnp.where(to_x // 2 == 0, 1, 3), jnp.where(to_x % 2 == 0, c, 0))
         return jnp.where(c == 0, 0, half_way)
 
-    def copies2():
+    def copies2(cols):
         out = []
         for d in range(16):
             to = (f + d) % 16
@@ -252,7 +243,7 @@
             c = turn(to_y)
             block = ((z_hi + c) % 4) * 4 + to_x
             to_z = ((z_hi + moved(c, to_x)) % 4) * 2 + z_lo
-            copy = t_copy(2, leaving.at[1, rows(block * 16, 16), :], arrived.at[2, rows(f * 16, 16), :], place(to_x, to_y, to_z, k))
+            copy = t_copy(2, leaving.at[1, rows(block * 16, 16), cols], arrived.at[2, rows(f * 16, 16), cols], place(to_x, to_y, to_z, k))
             out.append((d == 0, copy))
         return out
 
@@ -264,15 +255,15 @@
     to_hi = (from_hi + my_turn) % 4
     at_home = jnp.logical_and(z_hi == to_hi, k == x // 2)
 
-    def copies3():
+    def copies3(cols):
         out = []
         for dx in range(4):
             for dy in range(4):
                 to_x, to_y = (x + dx) % 4, (y + dy) % 4
                 copy = t_copy(
                     3,
-                    leaving.at[2, rows((to_x * 4 + to_y) * 16, 16), :],
-                    arrived.at[3, rows(slot3 * 16, 16), :],
+                    leaving.at[2, rows((to_x * 4 + to_y) * 16, 16), cols],
+                    arrived.at[3, rows(slot3 * 16, 16), cols],
                     place(to_x, to_y, to_hi * 2 + z_lo, x // 2),
                 )
                 out.append((dx == 0 and dy == 0, copy))
@@ -282,13 +273,34 @@
         pl.when(kept)(lambda: act(t_total(stage, 240)))
         pl.when(jnp.logical_not(kept))(lambda: act(t_total(stage, 256)))
 
-    def send_all(copies, kept, keep):
+    def send_all(copies, kept):
         for maybe_self, copy in copies:
             if maybe_self:
                 pl.when(jnp.logical_not(kept))(copy.start)
-                pl.when(kept)(keep)
             else:
                 copy.start()
+
+    def keep2():
+        arrived[2, rows(f * 16, 16), :] = leaving[1, rows((((z_hi + my_turn) % 4) * 4 + x) * 16, 16), :]
+
+    def keep3():
+        arrived[3, rows(slot3 * 16, 16), :] = leaving[2, rows(f * 16, 16), :]
+
+    def leave1(cols):
+        order = one_hot(lambda o: ((o // 128) * 4 + o % 4) * 32 + ((o // 4) % 4) * 8 + (o // 16) % 8)
+        leaving[0, :, cols] = dot(order, stream[:, cols].astype(BF16)).astype(BF16)
+        if cols.start == 0:
+            pl.semaphore_wait(hello.at[2], 1)
+        start_all(copies1(cols))
+
+    def leave2(cols):
+        leaving[1, :, cols] = stream[:, cols].astype(BF16)
+        send_all(copies2(cols), stays)
+
+    def leave3(cols):
+        order = one_hot(lambda o: ((o // 64) * 4 + (o // 4) % 4) * 16 + (o % 4) * 4 + (o // 16) % 4)
+        leaving[2, :, cols] = dot(order, stream[:, cols].astype(BF16)).astype(BF16)
+        send_all(copies3(cols), at_home)
 
     def pair_copy(p, index, src, dst):
         return pltpu.make_async_remote_copy(
@@ -303,8 +315,10 @@
     def share_copy(p):
         return pair_copy(p, 0, normed.at[p, 0:ROWS, :], normed.at[p, ROWS : 2 * ROWS, :])
 
-    def return_copy(p):
-        return pair_copy(p, 1, partial.at[p], partial_in.at[p])
+    halves = (slice(0, D // 2), slice(D // 2, D))
+
+    def return_copy(p, half):
+        return pair_copy(p, 1 + half, partial.at[p, :, halves[half]], partial_in.at[p, :, halves[half]])
 
     def greet(stage, peers):
         for peer in peers:
@@ -317,12 +331,12 @@
 
     def project(p, d, r):
         tokens = normed[p, r, :]
-        both_heads = dot(tokens, jnp.concatenate([w_attn[p, d, 0], w_attn[p, d, 1]], axis=1))
+        both_heads = dot(tokens, w_attn[p, d, :, 0:256])
         a, b = iotas((256, 256))
         gain = jnp.concatenate([qk_gain[p, 0:1, :] * 0.125] * 2 + [qk_gain[p, 1:2, :]] * 2, axis=1)
         sums = jnp.where(a // 64 == b // 64, 1.0 / 64.0, 0.0).astype(BF16)
         mean = dot((both_heads * both_heads).astype(BF16), sums)
-        qkv[r, 256:384] = dot(tokens, w_attn[p, d, 2]).astype(BF16)
+        qkv[r, 256:384] = dot(tokens, w_attn[p, d, :, 256:384]).astype(BF16)
         qkv[r, 0:256] = (both_heads * lax.rsqrt(mean + 1e-6) * gain).astype(BF16)
 
     def attend(d, r):
@@ -336,8 +350,7 @@
             results.append(summed[:, :128] / summed[:, 128:])
         heads[r, d * 128 : d * 128 + 128] = jnp.where(left, results[0], results[1]).astype(BF16)
 
-    def attention(p, relay0=None, relay1=None, relay3=None):
-        own_in(p)
+    def attention(p, after, relay0=None, relay1=None, relay3=None):
         project(p, 0, own)
         attend(0, own)
         share_copy(p).wait_recv()
@@ -355,11 +368,10 @@
         weights_in(p, 2)
         project(p, 2, other)
         attend(2, other)
-        partial[p] = dot(heads[other, :], w_out[p]).astype(BF16)
-        return_copy(p).start()
+        give(p, heads, w_out.at[p])
         project(p, 2, own)
         attend(2, own)
-        finish(p, heads, w_out[p])
+        finish(p, heads, w_out.at[p], after)
 
     def mlp_quarter(d, r):
         tokens = normed[3, r, :]
@@ -367,34 +379,40 @@
         up = dot(tokens, w_in[d, 1])
         hidden[r, d * 256 : d * 256 + 256] = (gate / (1.0 + jnp.exp(-gate)) * up).astype(BF16)
 
-    def mlp():
-        own_in(3)
-        mlp_quarter(0, own)
+    def mlp(after):
+        weights_in(3, 1)
+        for d in (0, 1):
+            mlp_quarter(d, own)
         share_copy(3).wait_recv()
-        mlp_quarter(0, other)
-        for d in (1, 3):
-            weights_in(3, d)
-            mlp_quarter(d, all_rows)
+        for d in (0, 1):
+            mlp_quarter(d, other)
+        weights_in(3, 3)
+        mlp_quarter(3, all_rows)
         weights_in(3, 2)
         mlp_quarter(2, other)
-        partial[3] = dot(hidden[other, :], w_down[...]).astype(BF16)
-        return_copy(3).start()
+        give(3, hidden, w_down)
         mlp_quarter(2, own)
-        finish(3, hidden, w_down[...])
-
-    def finish(p, left_ref, right_ref):
-        stream[...] = stream[...] + dot(left_ref[own, :], right_ref)
-        return_copy(p).wait_recv()
-        stream[...] = stream[...] + partial_in[p].astype(F32)
+        finish(3, hidden, w_down, after)
+
+    def give(p, left_ref, right_ref):
+        for half, cols in enumerate(halves):
+            partial[p, :, cols] = dot(left_ref[other, :], right_ref[:, cols]).astype(BF16)
+            return_copy(p, half).start()
+
+    def finish(p, left_ref, right_ref, after):
+        for half, cols in enumerate(halves):
+            summed = stream[:, cols] + dot(left_ref[own, :], right_ref[:, cols])
+            return_copy(p, half).wait_recv()
+            stream[:, cols] = summed + partial_in[p, :, cols].astype(F32)
+            after(cols)
 
     def begin(p):
         normed[p, 0:ROWS, :] = rms(stream[...], norm_gain[p : p + 1, :]).astype(BF16)
         share_copy(p).start()
 
+    tokens_in.start()
     for p in range(4):
-        own_copy(p, 0).start()
-        own_copy(p, 1).start()
-    own_rows.start()
+        start_all(own_copies(p))
     barrier = pltpu.get_barrier_semaphore()
     greeted = [place((x + e) % 4, y, z, k) for e in (1, 2, 3)]
     greeted += [{"ta": x, "ha": h, "wa": (w + d) % 8} for d in range(1, 8)]
@@ -402,10 +420,15 @@
     for peer in greeted:
         pl.semaphore_signal(barrier, inc=1, device_id=peer, device_id_type=MESH)
     pl.semaphore_wait(barrier, len(greeted))
+    tokens_in.wait()
     start_all(copies0())
+    own_in(0)
     x_send(0, 0)
     x_send(0, 1)
     greet(0, [place(x, y, (z + 1) % 8, k), place(x, y, (z + 7) % 8, k)])
+    own_in(1)
+    own_in(2)
+    arrived[0, rows(w * 32, 32), :] = tok_in[rows(y * 64 + z_lo * 32, 32), :]
 
     a, b = iotas((ROWS, ROWS))
     mask[...] = jnp.where((a // 8) % 4 == (b // 8) % 4, 1.0, 0.0).astype(BF16)
@@ -413,7 +436,6 @@
     greet(1, [place(x, y, (z + 2) % 8, k), place(x, y, (z + 6) % 8, k)])
     forward_y(0, 1, 3)
     x_send(1, 0)
-    own_rows.wait()
     t_total(0, 224).wait_recv()
     stream[...] = arrived[0].astype(F32)
     begin(0)
@@ -427,10 +449,10 @@
         forward_y(0, 2)
         relay_y(0, 3)
         split_in()
+        relay_y(0, 2)
+        forward_z(0, 2)
 
     def relays01():
-        forward_z(0, 2)
-        relay_y(0, 2)
         forward_y(1, 1, 3)
         x_send(2, 0)
 
@@ -438,12 +460,8 @@
         forward_z(1, 1, 3)
         x_send(2, 1)
 
-    attention(0, relays00, relays01, relays02)
-    pl.semaphore_wait(hello.at[2], 1)
-
-    order = one_hot(lambda o: ((o // 128) * 4 + o % 4) * 32 + ((o // 4) % 4) * 8 + (o // 16) % 8)
-    leaving[0] = dot(order, stream[...].astype(BF16)).astype(BF16)
-    start_all(copies1())
+    attention(0, leave1, relays00, relays01, relays02)
+
     own_block = z_lo * 8 + z_hi * 2 + k
     arrived[1, rows(group * 16, 16), :] = leaving[0, rows(own_block * 16, 16), :]
     a, b = iotas((ROWS, ROWS))
@@ -466,14 +484,9 @@
         forward_y(3, 1, 3)
         forward_z(2, 2)
 
-    attention(1, None, None, relays12)
-
-    leaving[1] = stream[...].astype(BF16)
-
-    def keep2():
-        arrived[2, rows(f * 16, 16), :] = leaving[1, rows((((z_hi + my_turn) % 4) * 4 + x) * 16, 16), :]
-
-    send_all(copies2(), stays, keep2)
+    attention(1, leave2, None, None, relays12)
+
+    pl.when(stays)(keep2)
     a, b = iotas((ROWS, ROWS))
     mask[...] = jnp.where(jnp.logical_and(a % 16 == b % 16, b // 16 <= a // 16), 1.0, 0.0).astype(BF16)
     relay_y(2, 2)
@@ -488,17 +501,12 @@
         forward_z(3, 2)
         relay_y(3, 2)
 
-    attention(2, None, None, relays21)
+    attention(2, lambda cols: None, None, None, relays21)
 
     begin(3)
-    mlp()
-
-    order = one_hot(lambda o: ((o // 64) * 4 + (o // 4) % 4) * 16 + (o % 4) * 4 + (o // 16) % 4)
-    leaving[2] = dot(order, stream[...].astype(BF16)).astype(BF16)
-    def keep3():
-        arrived[3, rows(slot3 * 16, 16), :] = leaving[2, rows(f * 16, 16), :]
-
-    send_all(copies3(), at_home, keep3)
+    mlp(leave3)
+
+    pl.when(at_home)(keep3)
     unless(at_home, 3, lambda copy: copy.wait_recv())
     order = one_hot(lambda o: (((o // 32) % 2) * 8 + o % 8) * 16 + (o // 64) * 4 + (o // 8) % 4)
     out_ref[...] = dot(order, arrived[3]).astype(BF16)
@@ -511,7 +519,8 @@
         for _ in range(3):
             w_total(p, 0, 0, 8).wait_send()
         share_copy(p).wait_send()
-        return_copy(p).wait_send()
+        return_copy(p, 0).wait_send()
+        return_copy(p, 1).wait_send()
 
 
 def local(tokens, norm_gain, qkv_weight, qk_gain, out_weight, ffn_in, ffn_out):
@@ -519,11 +528,11 @@
     vmem, hbm = pl.BlockSpec(memory_space=pltpu.VMEM), pl.BlockSpec(memory_space=pl.ANY)
     result = pl.pallas_call(
         kernel,
-        out_shape=jax.ShapeDtypeStruct((ROWS, D), BF16),
+        out_shape=pltpu.VMEM((ROWS, D), BF16),
         in_specs=[hbm, hbm, hbm, hbm, hbm, vmem, vmem],
         out_specs=vmem,
         scratch_shapes=[
-            pltpu.VMEM((3, 4, 3, D, 128), BF16),
+            pltpu.VMEM((3, 4, D, 384), BF16),
             pltpu.VMEM((3, 512, D), BF16),
             pltpu.VMEM((4, 2, D, 256), BF16),
             pltpu.VMEM((D, D), BF16),
@@ -538,13 +547,14 @@
             pltpu.VMEM((2 * ROWS, D), BF16),
             pltpu.VMEM((ROWS, ROWS), BF16),
             pltpu.VMEM((D, 2, 256), BF16),
+            pltpu.VMEM((ROWS, D), BF16),
             pltpu.SemaphoreType.DMA((4,)),
             pltpu.SemaphoreType.DMA((4, 4, 5)),
-            pltpu.SemaphoreType.DMA((5, 2)),
+            pltpu.SemaphoreType.DMA((5, 4)),
             pltpu.SemaphoreType.DMA((4,)),
             pltpu.SemaphoreType.DMA((4,)),
-            pltpu.SemaphoreType.DMA((4, 2)),
-            pltpu.SemaphoreType.DMA((4, 2)),
+            pltpu.SemaphoreType.DMA((4, 3)),
+            pltpu.SemaphoreType.DMA((4, 3)),
             pltpu.SemaphoreType.REGULAR((3,)),
         ],
         compiler_params=pltpu.CompilerParams(collective_id=0, has_side_effects=True, vmem_limit_bytes=60 * 2**20),

time: 112 us -> 110 us (0.982)
  no operation moved by 1% of the time
where the time goes in v4:
time: 110 us; the launch traced here: 108 us
  Pallas kernels  107 us (97%)
    pallas_call x1, Pallas kernels, local(): pl.pallas_call(kernel, out_shape=pltpu.VMEM((ROWS, D), BF16), in_specs=[h...  107 us

profile of v4, /device:TPU:6, one launch (start us, length us, event | category | flops | bytes accessed | tf_op | source)
XLA Modules:
  0.0 107.8 jit_solution(12840660150752343091)
XLA Ops:
  0.0 107.0 %shard_map.73 = bf16[256,1024]{1,0:T(8,128)(2,1)S(1)} custom-call(bf16[256,1024]{1,0:T(8,128)(2,1)} %bitcast.5, bf16[3,3,1024,256]{3,2,1,0:T(8,128)(2,1)} %bitcast.4, bf16[3,256,1024]{2,1,0:T(8,128)(2,1)} %out_src.1, bf16[1024,2,512]{2,1,0:T(2,128)(2,1)} %in_src.1, bf16[512,1024]{1,0:T(8,128)(2,1)} %down_src.1, f32[4,1024]{1,0:T(4,128)} %norm_gain.1, ...), custom_call_target="tpu_custom_call" | custom-call | tf_op jit(solution)/shard_map/pallas_call | solution.py:529
  107.0 0.8 copy.9
